TPU v7x, 32 devices: a whole 2x2x4 slice. The times are simulated.
32 devices in a mesh: pair: 4 (over y, x), virt: 8 (over z, core).
Axes of the slice: x: 2, y: 2, z: 4, core: 2. Of those that a mesh axis runs over, the one named last changes fastest.
Arguments:
- density_row_blocks: bfloat16 [160, 128, 2744], P('pair', 'virt'), may hold values from -6 to 6
- vir_left: bfloat16 [128, 2744], P('virt'), may hold values from -0.046875 to 0.046875
- vir_right: bfloat16 [128, 2744], P('virt'), may hold values from -0.109375 to 0.109375
- orb_energy: bfloat16 [128], P('virt'), may hold values from 0.5 to 3
- state_energy: float32 [8], replicated, may hold values from -1 to -0.1
- bra_ket_states: int32 [160, 2], P('pair'), may hold values from 0 to 7
- row_block_starts: int32 [160], P('pair'), may hold values from 0 to 2616
Outputs:
- slot_couplings: float32 [160], P('pair')
- heff: float32 [8, 8], replicated
All inputs are finite; a program needn't handle non-finite values.
Results may differ from a plain program's by a relative error of at most 0.0003.
Values may be sent and summed in bfloat16 or wider, within the bound.
A program may use at most 64 MiB of HBM per device.

v0:
```python
import jax
import jax.numpy as jnp
from jax import lax
from jax.sharding import PartitionSpec as P


def local(
    density_row_blocks,
    vir_left,
    vir_right,
    orb_energy,
    state_energy,
    bra_ket_states,
    row_block_starts,
):
    slots, rows, ntrip = density_row_blocks.shape
    nstate = state_energy.shape[0]
    virt_index = lax.axis_index("virt")
    positions = (
        row_block_starts[:, None] + virt_index * rows + jnp.arange(rows, dtype=jnp.int32)[None, :]
    )
    positions = positions.reshape(slots * rows)
    flat_rdm = density_row_blocks.reshape(slots * rows, ntrip)
    states = jnp.arange(nstate, dtype=jnp.int32)
    first = (bra_ket_states[:, 0:1] == states[None, :]).astype(jnp.float32)
    second = (bra_ket_states[:, 1:2] == states[None, :]).astype(jnp.float32)
    shift = jnp.dot(first + second, state_energy, precision=lax.Precision.HIGHEST)
    columns = jnp.take(lax.all_gather(vir_left, "virt", axis=0, tiled=True), positions, axis=1)
    right_piece = lax.all_gather(vir_right, "virt", axis=0, tiled=True)
    count = right_piece.shape[0]
    contracted = lax.dot_general(
        right_piece, flat_rdm, (((1,), (1,)), ((), ())), preferred_element_type=jnp.float32
    )
    inverse = 1.0 / (
        lax.all_gather(orb_energy, "virt", axis=0, tiled=True).astype(jnp.float32)[:, None]
        - shift[None, :]
    )
    product = columns.astype(jnp.float32).reshape(count, slots, rows) * contracted.reshape(
        count, slots, rows
    )
    partial_sums = jnp.sum(jnp.sum(product, axis=2) * inverse, axis=0)
    couplings = lax.psum(partial_sums, "virt")
    local_sum = jnp.dot(first.T, couplings[:, None] * second, precision=lax.Precision.HIGHEST)
    collected = lax.all_gather(local_sum[None], "pair", axis=0, tiled=True)
    coupling_sum = jnp.sum(collected, axis=0)
    heff = jnp.diag(state_energy) + 0.5 * (coupling_sum + coupling_sum.T)
    return (couplings, heff)


def solution(mesh):
    placed = (
        P("pair", "virt", None),
        P("virt", None),
        P("virt", None),
        P("virt"),
        P(),
        P("pair", None),
        P("pair"),
    )
    return jax.shard_map(
        local, mesh=mesh, in_specs=placed, out_specs=(P("pair"), P()), check_vma=False
    )
```

profile of v0, /device:TPU:0, one launch (start us, length us, event | category | flops | bytes accessed | tf_op | source)
XLA Modules:
  0.0 82.9 jit_solution(17060475857912333870)
XLA Ops:
  0.6 0.0 copy-start
  0.6 0.7 broadcast_add_fusion
  1.3 0.1 copy.22
  1.4 0.1 add.74
  1.5 17.2 %all_gather.12 = bf16[128,2744]{1,0:T(8,128)(2,1)S(1)} all-gather(bf16[16,2744]{1,0:T(8,128)(2,1)} %param.8), channel_id=1, replica_groups=mesh['pair'=4,'virt'=8] {'virt'}, dimensions={0}, use_global_device_ids=true | all-gather | bytes 790272 | tf_op jit(solution)/shard_map/all_gather | solution.py:28
  18.8 0.4 copy.23
  19.1 2.0 %gather_fusion = bf16[640,128]{1,0:T(8,128)(2,1)S(1)} fusion(bf16[128,2744]{0,1:T(8,128)(2,1)S(1)} %copy.23, s32[1024]{0:T(1024)S(1)} %pad_clamp_fusion), kind=kCustom, calls=%fused_computation | custom fusion | bytes 330240 | tf_op jit(solution)/shard_map/jit(_take)/gather | solution.py:28
  21.1 0.0 copy-start.1
  21.2 0.0 copy-start.2
  21.2 0.0 copy-start.4
  21.2 0.0 copy-start.3
  21.2 0.0 copy-done
  21.2 15.5 %all_gather.13 = bf16[128,2744]{1,0:T(8,128)(2,1)S(1)} all-gather(bf16[16,2744]{1,0:T(8,128)(2,1)S(1)} %copy-done), channel_id=1, replica_groups=mesh['pair'=4,'virt'=8] {'virt'}, dimensions={0}, use_global_device_ids=true | all-gather | bytes 790272 | tf_op jit(solution)/shard_map/all_gather | solution.py:29
  36.7 3.8 %fusion.5 = f32[128,40]{0,1:T(8,128)S(1)} fusion(bf16[40,16,2744]{2,1,0:T(8,128)(2,1)} %param.7, bf16[128,2744]{1,0:T(8,128)(2,1)S(1)} %all_gather.13, bf16[128,40,16]{0,2,1:T(8,128)(2,1)S(1)} %bitcast.24, pred[40,16]{0,1:T(8,128)(4,1)S(1)} %compare_and_fusion), kind=kOutput, calls=%fused_computation.4 | convolution fusion | flops 449899520 | bytes 4399744 | tf_op jit(solution)/shard_map/dot_general | solution.py:31
  40.5 0.0 copy-done.1
  40.5 0.0 copy-done.2
  40.5 0.2 convolution_bitcast_fusion
  40.7 0.0 copy-done.4
  40.7 0.6 dynamic-slice
  42.0 0.0 copy-done.3
  42.0 0.2 dynamic-update-slice
  42.2 17.7 %all-reduce = bf16[128]{0:T(256)(128)(2,1)S(1)} all-reduce(bf16[128]{0:T(256)(128)(2,1)S(1)} %dynamic-update-slice), channel_id=1, replica_groups=mesh['pair'=4,'virt'=8] {'virt'}, use_global_device_ids=true, to_apply=%add | all-reduce | flops 128 | bytes 512
  60.0 0.2 multiply_reduce_fusion
  60.1 13.6 %psum.7 = f32[40]{0:T(128)S(1)} all-reduce(f32[40]{0:T(128)S(1)} %multiply_reduce_fusion), channel_id=1, replica_groups=mesh['pair'=4,'virt'=8] {'virt'}, use_global_device_ids=true, to_apply=%region_2.3 | all-reduce | flops 40 | bytes 320 | tf_op jit(solution)/shard_map/psum | solution.py:42
  73.7 0.0 copy-start.5
  73.7 0.3 fusion.9
  74.0 8.2 %all-gather = f32[32,8]{1,0:T(8,128)S(1)} all-gather(f32[8,8]{1,0:T(8,128)S(1)} %fusion.9), channel_id=2, replica_groups=mesh['pair'=4,'virt'=8] {'pair'}, dimensions={0}, use_global_device_ids=true | all-gather | bytes 1280 | tf_op jit(solution)/shard_map/all_gather | solution.py:44
  82.2 0.1 copy.26
  82.3 0.7 fusion.21
  82.9 0.0 copy-done.5
  (8 shorter events, 0.1 us)
Async XLA Ops:
  0.6 20.6 %copy-start = (bf16[16,2744]{1,0:T(8,128)(2,1)S(1)}, bf16[16,2744]{1,0:T(8,128)(2,1)}, u32[]{:S(2)}) copy-start(bf16[16,2744]{1,0:T(8,128)(2,1)} %param.9) | copy-start | bytes 263428
  21.1 19.3 %copy-start.1 = (s32[40,2]{0,1:T(2,128)S(1)}, s32[40,2]{0,1:T(2,128)}, u32[]{:S(2)}) copy-start(s32[40,2]{0,1:T(2,128)} %param.12) | copy-start | bytes 964
  21.2 19.3 %copy-start.2 = (f32[8]{0:T(128)S(1)}, f32[8]{0:T(128)}, u32[]{:S(2)}) copy-start(f32[8]{0:T(128)} %param.11) | copy-start | bytes 100
  21.2 19.5 %copy-start.4 = (u32[32]{0:T(128)S(1)}, u32[32]{0:T(128)}, u32[]{:S(2)}) copy-start(u32[32]{0:T(128)} %constant.33) | copy-start | bytes 388
  21.2 20.8 %copy-start.3 = (bf16[16]{0:T(256)(128)(2,1)S(1)}, bf16[16]{0:T(256)(128)(2,1)}, u32[]{:S(2)}) copy-start(bf16[16]{0:T(256)(128)(2,1)} %param.10) | copy-start | bytes 100
  73.7 9.2 %copy-start.5 = (f32[40]{0:T(128)}, f32[40]{0:T(128)S(1)}, u32[]{:S(2)}) copy-start(f32[40]{0:T(128)S(1)} %psum.7) | copy-start | bytes 484
where the time goes:
time: 83.2 us; the launch traced here: 82.9 us
  blocking collectives  72.2 us (87%)
  matrix products  4.26 us (5%)
  local copies, waits for them, and re-layouts  3.48 us (4%)
  other arithmetic  1.59 us (2%)
  between operations  1.41 us (2%)
    unnamed x1, blocking collectives  17.7 us
    all_gather x1, blocking collectives, local(): lax.all_gather(vir_left, 'virt', axis=0, tiled=True)  17.2 us
    all_gather x1, blocking collectives, local(): right_piece = lax.all_gather(vir_right, 'virt', axis=0, tiled=True)  15.5 us
    psum x1, blocking collectives, local(): couplings = lax.psum(partial_sums, 'virt')  13.6 us
    all_gather x1, blocking collectives, local(): collected = lax.all_gather(local_sum[None], 'pair', axis=0, tiled=True)  8.18 us
    dot_general x1, matrix products, local(): lax.dot_general(right_piece, flat_rdm, (((1,), (1,)), ((), ())), preferre...  3.8 us
    gather x1, local copies, waits for them, and re-layouts, local(): jnp.take(lax.all_gather(vir_left, 'virt', axis=0, tiled=True), positions,...  1.99 us

commit v1 on v0

--- a/solution.py
+++ b/solution.py
@@ -39,7 +39,10 @@
         count, slots, rows
     )
     partial_sums = jnp.sum(jnp.sum(product, axis=2) * inverse, axis=0)
-    couplings = lax.psum(partial_sums, "virt")
+    size, couplings = (lax.axis_size("virt"), partial_sums)
+    for far in [1 << k for k in range(size.bit_length() - 1)]:
+        pairs = [(i, i ^ far) for i in range(size)]
+        couplings = couplings + lax.ppermute(couplings, "virt", pairs)
     local_sum = jnp.dot(first.T, couplings[:, None] * second, precision=lax.Precision.HIGHEST)
     collected = lax.all_gather(local_sum[None], "pair", axis=0, tiled=True)
     coupling_sum = jnp.sum(collected, axis=0)

time: 83.2 us -> 81 us (0.974)
  blocking collectives: 72.2 us -> 58.8 us
  waiting for transfers between devices: 0 us -> 9.18 us
  local copies, waits for them, and re-layouts: 3.48 us -> 5.44 us
    psum x1 -> x0, blocking collectives: 13.6 us -> none  [local(): couplings = lax.psum(partial_sums, 'virt')]
    ppermute x0 -> x3, waiting for transfers between devices: none -> 9.18 us  [local(): couplings = couplings + lax.ppermute(couplings, 'virt', pairs)]
    unnamed x15 -> x7, local copies, waits for them, and re-layouts: 0.89 us -> 2.11 us
  transfers between devices with their start and end apart: 0 -> 3, of which waited for: 0 -> 3; matrix products, arithmetic and copies ran while one was open for 0% -> 0% of each run, Pallas kernels for 0% -> 0%
where the time goes in v1:
time: 81 us; the launch traced here: 80.7 us
  blocking collectives  58.8 us (73%)
  waiting for transfers between devices  9.18 us (11%)
  local copies, waits for them, and re-layouts  5.44 us (7%)
  matrix products  4.28 us (5%)
  other arithmetic  1.57 us (2%)
  between operations  1.36 us (2%)
    unnamed x1, blocking collectives  17.7 us
    all_gather x1, blocking collectives, local(): lax.all_gather(vir_left, 'virt', axis=0, tiled=True)  17.2 us
    all_gather x1, blocking collectives, local(): right_piece = lax.all_gather(vir_right, 'virt', axis=0, tiled=True)  15.7 us
    ppermute x3, waiting for transfers between devices, local(): couplings = couplings + lax.ppermute(couplings, 'virt', pairs)  9.18 us
    all_gather x1, blocking collectives, local(): collected = lax.all_gather(local_sum[None], 'pair', axis=0, tiled=True)  8.19 us
    dot_general x1, matrix products, local(): lax.dot_general(right_piece, flat_rdm, (((1,), (1,)), ((), ())), preferre...  3.82 us
    unnamed x7, local copies, waits for them, and re-layouts  2.11 us
    gather x1, local copies, waits for them, and re-layouts, local(): jnp.take(lax.all_gather(vir_left, 'virt', axis=0, tiled=True), positions,...  1.98 us
  transfers between devices with their start and end apart: 3, of which 3 were waited for; matrix products, arithmetic and copies ran while one was open for 0% of the time, Pallas kernels for 0%

profile of v1, /device:TPU:0, one launch (start us, length us, event | category | flops | bytes accessed | tf_op | source)
XLA Modules:
  0.0 80.7 jit_solution(3836860676254951525)
XLA Ops:
  0.6 0.0 copy-start
  0.6 0.7 broadcast_add_fusion
  1.3 0.1 copy.22
  1.4 0.1 add.81
  1.5 17.2 %all_gather.12 = bf16[128,2744]{1,0:T(8,128)(2,1)S(1)} all-gather(bf16[16,2744]{1,0:T(8,128)(2,1)} %param.8), channel_id=1, replica_groups=mesh['pair'=4,'virt'=8] {'virt'}, dimensions={0}, use_global_device_ids=true | all-gather | bytes 790272 | tf_op jit(solution)/shard_map/all_gather | solution.py:28
  18.8 0.4 copy.23
  19.1 15.7 %all_gather.13 = bf16[128,2744]{1,0:T(8,128)(2,1)S(1)} all-gather(bf16[16,2744]{1,0:T(8,128)(2,1)} %param.9), channel_id=1, replica_groups=mesh['pair'=4,'virt'=8] {'virt'}, dimensions={0}, use_global_device_ids=true | all-gather | bytes 790272 | tf_op jit(solution)/shard_map/all_gather | solution.py:29
  34.8 0.8 slice_bitcast_fusion.1
  35.5 1.2 %dynamic-slice = u32[1]{0:T(128)} dynamic-slice(u32[32]{0:T(128)} %constant.33, u32[]{:T(128)S(6)} %add.90), dynamic_slice_sizes={1} | dynamic-slice | bytes 12
  37.4 0.9 %dynamic-update-slice = bf16[128]{0:T(256)(128)(2,1)S(1)} dynamic-update-slice(bf16[128]{0:T(256)(128)(2,1)S(1)} %broadcast.43, bf16[16]{0:T(256)(128)(2,1)} %param.10, u32[]{:T(128)} %bitcast.3) | dynamic-update-slice | bytes 68
  38.3 17.7 %all-reduce = bf16[128]{0:T(256)(128)(2,1)S(1)} all-reduce(bf16[128]{0:T(256)(128)(2,1)S(1)} %dynamic-update-slice), channel_id=1, replica_groups=mesh['pair'=4,'virt'=8] {'virt'}, use_global_device_ids=true, to_apply=%add | all-reduce | flops 128 | bytes 512
  56.0 2.0 %gather_fusion = bf16[640,128]{1,0:T(8,128)(2,1)S(1)} fusion(bf16[128,2744]{0,1:T(8,128)(2,1)S(1)} %copy.23, s32[1024]{0:T(1024)S(1)} %pad_clamp_fusion), kind=kCustom, calls=%fused_computation | custom fusion | bytes 330240 | tf_op jit(solution)/shard_map/jit(_take)/gather | solution.py:28
  58.0 0.0 copy-done
  58.0 0.2 convolution_bitcast_fusion
  58.2 3.8 %fusion.5 = f32[128,40]{0,1:T(8,128)S(1)} fusion(bf16[40,16,2744]{2,1,0:T(8,128)(2,1)} %param.7, bf16[128,2744]{1,0:T(8,128)(2,1)S(1)} %all_gather.13, bf16[128,40,16]{0,2,1:T(8,128)(2,1)S(1)} %bitcast.24, pred[40,16]{0,1:T(8,128)(4,1)S(1)} %compare_and_fusion), kind=kOutput, calls=%fused_computation.4 | convolution fusion | flops 449899520 | bytes 4399744 | tf_op jit(solution)/shard_map/dot_general | solution.py:31
  62.1 0.2 multiply_reduce_fusion
  62.3 0.1 collective-permute-start
  62.3 1.1 %collective-permute-done = f32[40]{0:T(128)S(1)} collective-permute-done((f32[40]{0:T(128)S(1)}, f32[40]{0:T(128)S(1)}, u32[]{:S(2)}, u32[]{:S(2)}) %collective-permute-start) | collective-permute-done | bytes 192 | tf_op jit(solution)/shard_map/ppermute | solution.py:45
  63.5 0.0 collective-permute-start.1
  63.5 3.6 %collective-permute-done.1 = f32[40]{0:T(128)S(1)} collective-permute-done((f32[40]{0:T(128)S(1)}, f32[40]{0:T(128)S(1)}, u32[]{:S(2)}, u32[]{:S(2)}) %collective-permute-start.1) | collective-permute-done | bytes 192 | tf_op jit(solution)/shard_map/ppermute | solution.py:45
  67.1 0.0 collective-permute-start.2
  67.1 4.5 %collective-permute-done.2 = f32[40]{0:T(128)S(1)} collective-permute-done((f32[40]{0:T(128)S(1)}, f32[40]{0:T(128)S(1)}, u32[]{:S(2)}, u32[]{:S(2)}) %collective-permute-start.2) | collective-permute-done | bytes 192 | tf_op jit(solution)/shard_map/ppermute | solution.py:45
  71.5 0.0 copy-start.1
  71.5 0.3 fusion.9
  71.8 8.2 %all-gather = f32[32,8]{1,0:T(8,128)S(1)} all-gather(f32[8,8]{1,0:T(8,128)S(1)} %fusion.9), channel_id=2, replica_groups=mesh['pair'=4,'virt'=8] {'pair'}, dimensions={0}, use_global_device_ids=true | all-gather | bytes 1280 | tf_op jit(solution)/shard_map/all_gather | solution.py:47
  80.0 0.1 copy.26
  80.1 0.7 fusion.21
  80.7 0.0 copy-done.1
  (10 shorter events, 0.1 us)
Async XLA Ops:
  0.6 57.4 %copy-start = (f32[8]{0:T(128)S(1)}, f32[8]{0:T(128)}, u32[]{:S(2)}) copy-start(f32[8]{0:T(128)} %param.11) | copy-start | bytes 100
  62.3 1.2 %collective-permute-start = (f32[40]{0:T(128)S(1)}, f32[40]{0:T(128)S(1)}, u32[]{:S(2)}, u32[]{:S(2)}) collective-permute-start(f32[40]{0:T(128)S(1)} %multiply_reduce_fusion), channel_id=1, source_target_pairs={{0,1},{1,0},{2,3},{3,2},{4,5},{5,4},{6,7},{7,6},{8,9},{9,8},{10,11... | collective-permute-start | bytes 488 | tf_op jit(solution)/shard_map/ppermute | solution.py:45
  63.5 3.6 %collective-permute-start.1 = (f32[40]{0:T(128)S(1)}, f32[40]{0:T(128)S(1)}, u32[]{:S(2)}, u32[]{:S(2)}) collective-permute-start(f32[40]{0:T(128)S(1)} %add.85), channel_id=1, source_target_pairs={{0,2},{1,3},{2,0},{3,1},{4,6},{5,7},{6,4},{7,5},{8,10},{9,11},{10,... | collective-permute-start | bytes 488 | tf_op jit(solution)/shard_map/ppermute | solution.py:45
  67.1 4.5 %collective-permute-start.2 = (f32[40]{0:T(128)S(1)}, f32[40]{0:T(128)S(1)}, u32[]{:S(2)}, u32[]{:S(2)}) collective-permute-start(f32[40]{0:T(128)S(1)} %add.86), channel_id=1, source_target_pairs={{0,4},{1,5},{2,6},{3,7},{4,0},{5,1},{6,2},{7,3},{8,12},{9,13},{10,... | collective-permute-start | bytes 488 | tf_op jit(solution)/shard_map/ppermute | solution.py:45
  71.5 9.2 %copy-start.1 = (f32[40]{0:T(128)}, f32[40]{0:T(128)S(1)}, u32[]{:S(2)}) copy-start(f32[40]{0:T(128)S(1)} %add.87) | copy-start | bytes 484

commit v2 on v0

--- a/solution.py
+++ b/solution.py
@@ -41,7 +41,17 @@
     partial_sums = jnp.sum(jnp.sum(product, axis=2) * inverse, axis=0)
     couplings = lax.psum(partial_sums, "virt")
     local_sum = jnp.dot(first.T, couplings[:, None] * second, precision=lax.Precision.HIGHEST)
-    collected = lax.all_gather(local_sum[None], "pair", axis=0, tiled=True)
+    inputs = local_sum[None]
+    world_n = lax.psum(1, "pair")
+    z1 = sorted(((num, (num + 1) % world_n) for num in range(world_n)))
+    mat_out = inputs
+    ledger = [mat_out]
+    for to_i in range(1, world_n):
+        mat_out = lax.ppermute(mat_out, "pair", z1)
+        ledger.insert(0, mat_out)
+    value_now = jnp.concatenate(ledger, 0)
+    r1 = lax.axis_index("pair") + 1
+    collected = jnp.roll(value_now, r1 * inputs.shape[0], 0)
     coupling_sum = jnp.sum(collected, axis=0)
     heff = jnp.diag(state_energy) + 0.5 * (coupling_sum + coupling_sum.T)
     return (couplings, heff)

time: 83.2 us -> 90.7 us (1.090)
  waiting for transfers between devices: 0 us -> 11.4 us
  blocking collectives: 72.2 us -> 64.2 us
  starting transfers between devices: 0 us -> 2.08 us
  local copies, waits for them, and re-layouts: 3.48 us -> 5.46 us
    ppermute x0 -> x3, waiting for transfers between devices: none -> 11.4 us  [local(): mat_out = lax.ppermute(mat_out, 'pair', z1)]
    all_gather x1 -> x0, blocking collectives: 8.18 us -> none  [local(): collected = lax.all_gather(local_sum[None], 'pair', axis=0, tiled=True)]
    ppermute x0 -> x3, starting transfers between devices: none -> 2.08 us  [local(): mat_out = lax.ppermute(mat_out, 'pair', z1)]
    unnamed x15 -> x14, local copies, waits for them, and re-layouts: 0.89 us -> 2.12 us
  transfers between devices with their start and end apart: 0 -> 3, of which waited for: 0 -> 3; matrix products, arithmetic and copies ran while one was open for 0% -> 0% of each run, Pallas kernels for 0% -> 0%
where the time goes in v2:
time: 90.7 us; the launch traced here: 90.5 us
  blocking collectives  64.2 us (71%)
  waiting for transfers between devices  11.4 us (13%)
  local copies, waits for them, and re-layouts  5.46 us (6%)
  matrix products  4.29 us (5%)
  starting transfers between devices  2.08 us (2%)
  other arithmetic  1.57 us (2%)
  between operations  1.4 us (2%)
    unnamed x1, blocking collectives  17.7 us
    all_gather x1, blocking collectives, local(): lax.all_gather(vir_left, 'virt', axis=0, tiled=True)  17.2 us
    all_gather x1, blocking collectives, local(): right_piece = lax.all_gather(vir_right, 'virt', axis=0, tiled=True)  15.7 us
    psum x1, blocking collectives, local(): couplings = lax.psum(partial_sums, 'virt')  13.6 us
    ppermute x3, waiting for transfers between devices, local(): mat_out = lax.ppermute(mat_out, 'pair', z1)  11.4 us
    dot_general x1, matrix products, local(): lax.dot_general(right_piece, flat_rdm, (((1,), (1,)), ((), ())), preferre...  3.82 us
    unnamed x14, local copies, waits for them, and re-layouts  2.12 us
    ppermute x3, starting transfers between devices, local(): mat_out = lax.ppermute(mat_out, 'pair', z1)  2.08 us
  transfers between devices with their start and end apart: 3, of which 3 were waited for; matrix products, arithmetic and copies ran while one was open for 0% of the time, Pallas kernels for 0%

profile of v2, /device:TPU:0, one launch (start us, length us, event | category | flops | bytes accessed | tf_op | source)
XLA Modules:
  0.0 90.5 jit_solution(8254686450895379442)
XLA Ops:
  0.6 0.0 copy-start
  0.6 0.7 broadcast_add_fusion
  1.3 0.1 copy.22
  1.4 0.1 add.87
  1.5 17.2 %all_gather.9 = bf16[128,2744]{1,0:T(8,128)(2,1)S(1)} all-gather(bf16[16,2744]{1,0:T(8,128)(2,1)} %param.8), channel_id=1, replica_groups=mesh['pair'=4,'virt'=8] {'virt'}, dimensions={0}, use_global_device_ids=true | all-gather | bytes 790272 | tf_op jit(solution)/shard_map/all_gather | solution.py:28
  18.8 0.4 copy.23
  19.1 15.7 %all_gather.10 = bf16[128,2744]{1,0:T(8,128)(2,1)S(1)} all-gather(bf16[16,2744]{1,0:T(8,128)(2,1)} %param.9), channel_id=1, replica_groups=mesh['pair'=4,'virt'=8] {'virt'}, dimensions={0}, use_global_device_ids=true | all-gather | bytes 790272 | tf_op jit(solution)/shard_map/all_gather | solution.py:29
  34.8 0.8 slice_bitcast_fusion.1
  35.6 1.2 %dynamic-slice = u32[1]{0:T(128)} dynamic-slice(u32[32]{0:T(128)} %constant.60, u32[]{:T(128)S(6)} %add.96), dynamic_slice_sizes={1} | dynamic-slice | bytes 12
  37.5 0.9 dynamic-update-slice
  38.3 17.7 %all-reduce = bf16[128]{0:T(256)(128)(2,1)S(1)} all-reduce(bf16[128]{0:T(256)(128)(2,1)S(1)} %dynamic-update-slice), channel_id=1, replica_groups=mesh['pair'=4,'virt'=8] {'virt'}, use_global_device_ids=true, to_apply=%add | all-reduce | flops 128 | bytes 512
  56.0 2.0 %gather_fusion = bf16[640,128]{1,0:T(8,128)(2,1)S(1)} fusion(bf16[128,2744]{0,1:T(8,128)(2,1)S(1)} %copy.23, s32[1024]{0:T(1024)S(1)} %pad_clamp_fusion), kind=kCustom, calls=%fused_computation | custom fusion | bytes 330240 | tf_op jit(solution)/shard_map/jit(_take)/gather | solution.py:28
  58.0 0.0 copy-done
  58.0 0.2 convolution_bitcast_fusion.1
  58.2 3.8 %fusion.5 = f32[128,40]{0,1:T(8,128)S(1)} fusion(bf16[40,16,2744]{2,1,0:T(8,128)(2,1)} %param.7, bf16[128,2744]{1,0:T(8,128)(2,1)S(1)} %all_gather.10, bf16[128,40,16]{0,2,1:T(8,128)(2,1)S(1)} %bitcast.24, pred[40,16]{0,1:T(8,128)(4,1)S(1)} %compare_and_fusion), kind=kOutput, calls=%fused_computation.4 | convolution fusion | flops 449899520 | bytes 4399744 | tf_op jit(solution)/shard_map/dot_general | solution.py:31
  62.1 0.2 multiply_reduce_fusion
  62.3 13.6 %psum.7 = f32[40]{0:T(128)S(1)} all-reduce(f32[40]{0:T(128)S(1)} %multiply_reduce_fusion), channel_id=1, replica_groups=mesh['pair'=4,'virt'=8] {'virt'}, use_global_device_ids=true, to_apply=%region_2.3 | all-reduce | flops 40 | bytes 320 | tf_op jit(solution)/shard_map/psum | solution.py:42
  75.9 0.0 copy-start.1
  75.9 0.3 convolution_bitcast_fusion
  76.1 1.5 %collective-permute-start = (f32[1,8,8]{2,1,0:T(8,128)S(1)}, f32[1,8,8]{2,1,0:T(8,128)S(1)}, u32[]{:S(2)}, u32[]{:S(2)}) collective-permute-start(f32[1,8,8]{2,1,0:T(8,128)S(1)} %convolution_bitcast_fusion), channel_id=1, source_target_pairs={{0,8},{8,16},{16,24},{24,0},{1,9},{9,17},{17,25},{25,1},{2,10},{10... | collective-permute-start | bytes 776 | tf_op jit(solution)/shard_map/ppermute | solution.py:50
  77.6 3.0 %collective-permute-done = f32[1,8,8]{2,1,0:T(8,128)S(1)} collective-permute-done((f32[1,8,8]{2,1,0:T(8,128)S(1)}, f32[1,8,8]{2,1,0:T(8,128)S(1)}, u32[]{:S(2)}, u32[]{:S(2)}) %collective-permute-start) | collective-permute-done | bytes 288 | tf_op jit(solution)/shard_map/ppermute | solution.py:50
  80.6 0.6 collective-permute-start.1
  81.2 3.9 %collective-permute-done.1 = f32[1,8,8]{2,1,0:T(8,128)S(1)} collective-permute-done((f32[1,8,8]{2,1,0:T(8,128)S(1)}, f32[1,8,8]{2,1,0:T(8,128)S(1)}, u32[]{:S(2)}, u32[]{:S(2)}) %collective-permute-start.1) | collective-permute-done | bytes 288 | tf_op jit(solution)/shard_map/ppermute | solution.py:50
  85.1 0.0 collective-permute-start.2
  85.1 4.5 %collective-permute-done.2 = f32[1,8,8]{2,1,0:T(8,128)S(1)} collective-permute-done((f32[1,8,8]{2,1,0:T(8,128)S(1)}, f32[1,8,8]{2,1,0:T(8,128)S(1)}, u32[]{:S(2)}, u32[]{:S(2)}) %collective-permute-start.2) | collective-permute-done | bytes 288 | tf_op jit(solution)/shard_map/ppermute | solution.py:50
  89.7 0.1 copy.26
  89.8 0.7 fusion.20
  90.5 0.0 copy-done.1
  (15 shorter events, 0.1 us)
Async XLA Ops:
  0.6 57.4 %copy-start = (f32[8]{0:T(128)S(1)}, f32[8]{0:T(128)}, u32[]{:S(2)}) copy-start(f32[8]{0:T(128)} %param.11) | copy-start | bytes 100
  75.9 14.6 %copy-start.1 = (f32[40]{0:T(128)}, f32[40]{0:T(128)S(1)}, u32[]{:S(2)}) copy-start(f32[40]{0:T(128)S(1)} %psum.7) | copy-start | bytes 484
  76.1 4.5 %collective-permute-start = (f32[1,8,8]{2,1,0:T(8,128)S(1)}, f32[1,8,8]{2,1,0:T(8,128)S(1)}, u32[]{:S(2)}, u32[]{:S(2)}) collective-permute-start(f32[1,8,8]{2,1,0:T(8,128)S(1)} %convolution_bitcast_fusion), channel_id=1, source_target_pairs={{0,8},{8,16},{16,24},{24,0},{1,9},{9,17},{17,25},{25,1},{2,10},{10... | collective-permute-start | bytes 776 | tf_op jit(solution)/shard_map/ppermute | solution.py:50
  80.6 4.5 %collective-permute-start.1 = (f32[1,8,8]{2,1,0:T(8,128)S(1)}, f32[1,8,8]{2,1,0:T(8,128)S(1)}, u32[]{:S(2)}, u32[]{:S(2)}) collective-permute-start(f32[1,8,8]{2,1,0:T(8,128)S(1)} %collective-permute-done), channel_id=1, source_target_pairs={{0,8},{8,16},{16,24},{24,0},{1,9},{9,17},{17,25},{25,1},{2,10},{10... | collective-permute-start | bytes 776 | tf_op jit(solution)/shard_map/ppermute | solution.py:50
  85.1 4.5 %collective-permute-start.2 = (f32[1,8,8]{2,1,0:T(8,128)S(1)}, f32[1,8,8]{2,1,0:T(8,128)S(1)}, u32[]{:S(2)}, u32[]{:S(2)}) collective-permute-start(f32[1,8,8]{2,1,0:T(8,128)S(1)} %collective-permute-done.1), channel_id=1, source_target_pairs={{0,8},{8,16},{16,24},{24,0},{1,9},{9,17},{17,25},{25,1},{2,10},{10... | collective-permute-start | bytes 776 | tf_op jit(solution)/shard_map/ppermute | solution.py:50
